TPU v7x, 32 devices: a whole 2x2x4 slice. The times are simulated.
32 devices in a mesh: groups: 2 (over x), expert: 8 (over z, y), dp: 2 (over core).
Axes of the slice: x: 2, y: 2, z: 4, core: 2. Of those that a mesh axis runs over, the one named last changes fastest.
Arguments:
- tokens: bfloat16 [128, 2880], P(('groups', 'expert', 'dp')), parts along dimension 0, may hold values from -6 to 6
- norm_gain: bfloat16 [2, 2880], replicated, may hold values from 0.25 to 1.75
- w_gate: bfloat16 [2, 2880, 23040], P(None, None, ('expert', 'dp')), may hold values from -0.109375 to 0.109375
- w_up: bfloat16 [2, 2880, 23040], P(None, None, ('expert', 'dp')), may hold values from -0.109375 to 0.109375
- w_down: bfloat16 [2, 23040, 2880], P(None, ('expert', 'dp')), may hold values from -0.109375 to 0.109375
- routes: int32 [2, 128, 4], P(None, ('groups', 'expert', 'dp')), parts along dimension 1, may hold values from 0 to 7, all different within a row; in each aligned block of 4 rows (0 to 3, 4 to 7, ..., all dimensions but the last counted through in order) at most 3 rows name the same one
- gates: float32 [2, 128, 4], P(None, ('groups', 'expert', 'dp')), parts along dimension 1, may hold values from 0.1 to 1
Outputs:
- mixed: bfloat16 [128, 2880], P(('groups', 'expert', 'dp')), parts along dimension 0
There are 2 independent parts, one for each index of `groups`. A program takes and returns all parts, laid end to end along the dimension named above; an argument that names none is the same for every part. Nothing has to cross between parts.
Inputs may be any that keep to these rules, and one draw needn't show every extreme that they name: `routes`: each token names 4 different experts; among the 4 rows of one device (aligned blocks of a layer) no expert is named more than 3 times, and in every layer some device's block names some expert exactly 3 times.
All inputs are finite; a program needn't handle non-finite values.
Results may differ from a plain program's by a relative error of at most 0.014.
Values may be sent and summed in bfloat16 or wider, within the bound.
A program may use at most 128 MiB of HBM per device.

v0:
```python
import functools

import jax
import jax.numpy as jnp
from jax import lax
from jax.experimental import pallas as pl
from jax.experimental.pallas import tpu as pltpu
from jax.sharding import PartitionSpec as P

MESH = pl.DeviceIdType.MESH
EPS = 1e-05
TILE = 512
PARTS = 2
CUTS = 1
CAP = 3
MXU = 256


def col_tiles(start, stop, width):
    tiles = []
    while start < stop:
        tiles.append((start, min(width, stop - start)))
        start += width
    return tiles


def tiled_loop(start, stop, width, body):
    full = (stop - start) // width
    if full > 1:
        @pl.loop(0, full)
        def _(i):
            body(pl.multiple_of(start + i * width, 128), width)
    elif full == 1:
        body(start, width)
    if (stop - start) % width:
        body(start + full * width, (stop - start) % width)


def dot_rows(left, right):
    return lax.dot_general(
        left, right, (((1,), (1,)), ((), ())), preferred_element_type=jnp.float32
    )


def folded(d_model):
    for main in range(MXU, d_model, MXU):
        pad = -(-(d_model - main) // 128) * 128
        if CAP * pad <= main and (CAP - 1) * pad % MXU == 0:
            return main, pad
    return None


def tiled(chips, chips_per_expert, rows, d_model, ff):
    tokens = 2 * chips * rows
    blocks = -(-ff // MXU)
    tails = (d_model % MXU, ff % MXU)
    return (
        chips <= 16
        and chips & (chips - 1) == 0
        and chips_per_expert == 1
        and rows == CAP + 1
        and folded(d_model) is not None
        and tokens % 16 == 0
        and blocks * (tokens // 4) <= 256
        and all(tail and tail % 16 == 0 for tail in tails)
        and tails[0] <= 128
    )


def filled(block, size):
    short = size - block.shape[0]
    if short == 0:
        return block
    return jnp.concatenate([block, jnp.zeros((short, block.shape[1]), block.dtype)], axis=0)


def kernel(
    chips, chips_per_expert, tok_hbm, gain_hbm, wg_hbm, wu_hbm, wd_hbm, routes_hbm, gates_hbm,
    out_ref,
    wg, wu, wd, gathered, stacked, x_buf, act, y_buf, y_half, peer_buf, blocks, back, hidden,
    w_sem, ag_send, ag_recv, fw_send, fw_recv, pr_send, pr_recv, rs_send, rs_recv,
    tok_ref, gain_ref, routes_ref, gates_ref, in_sem, *tails, accs=None,
):
    me = lax.axis_index("expert")
    core = lax.axis_index("dp")
    other = 1 - core
    layers, ff, d_model = wd_hbm.shape
    rows = tok_ref.shape[0]
    fast = accs is not None
    whole = d_model // MXU * MXU
    rest = d_model - whole
    strips = -(-ff // MXU)
    half = chips * rows
    step = -(-d_model // (128 * PARTS)) * 128
    parts = col_tiles(0, d_model, step)
    cuts = col_tiles(0, d_model, -(-d_model // (MXU * CUTS)) * MXU)
    if fast:
        main, pad = folded(d_model)
        cuts = [(0, main)]
        parts = [(0, (CAP - 1) * pad), ((CAP - 1) * pad, main - (CAP - 1) * pad)]
        pair_lanes = [(0, pad + parts[0][1]), (pad + parts[0][1], parts[1][1])]
    else:
        pair_lanes = parts

    if fast:
        wg_raw, wu_raw, wd_raw, wg_rest, wu_rest, wd_rest, packed, norm_buf, route_nums, slots = tails
        ups = ((wg_hbm, wg, wg_raw, wg_rest), (wu_hbm, wu, wu_raw, wu_rest))

    def strip_copy(layer, i, f):
        src, dst = ups[i][:2]
        height = pl.ds(f * MXU, min(MXU, ff - f * MXU))
        return pltpu.make_async_copy(
            src.at[layer, height, pl.ds(0, whole)], dst.at[layer, height, :], w_sem.at[layer, i, f]
        )

    def rest_copy(layer, i):
        src, raw = (ups[0][0], wg_raw) if i == 0 else (ups[1][0], wu_raw) if i == 1 else (wd_hbm, wd_raw)
        return pltpu.make_async_copy(
            src.at[layer, :, pl.ds(whole, rest)],
            raw.at[layer, pl.ds(0, ff), :],
            w_sem.at[layer, i, strips],
        )

    def down_copy(layer):
        return pltpu.make_async_copy(
            wd_hbm.at[layer, :, pl.ds(0, whole)], wd.at[layer], w_sem.at[layer, 2, 0]
        )

    def weights(layer):
        if fast:
            return (
                [rest_copy(layer, i) for i in range(2)]
                + [strip_copy(layer, i, f) for f in range(strips) for i in range(2)]
                + [rest_copy(layer, 2), down_copy(layer)]
            )
        pairs = ((wg_hbm, wg), (wu_hbm, wu), (wd_hbm, wd))
        return [
            pltpu.make_async_copy(src.at[layer], dst.at[layer], w_sem.at[layer, i])
            for i, (src, dst) in enumerate(pairs)
        ]

    def turn(layer, i, f):
        _, dst, raw, turned = ups[i]
        strip_copy(layer, i, f).wait()
        if f == 0:
            rest_copy(layer, i).wait()
        height = pl.ds(f * MXU, MXU)
        for k in range(whole // MXU):
            cols = pl.ds(k * MXU, MXU)
            dst[layer, height, cols] = dst[layer, height, cols].T
        turned[layer, :, height] = raw[layer, height, :].T

    def turn_all(layer, pieces):
        for i, f in pieces:
            turn(layer, i, f)

    def pad_down(layer):
        rest_copy(layer, 2).wait()
        wd_rest[layer] = jnp.zeros(wd_rest.shape[1:], wd_rest.dtype)
        wd_rest[layer, pl.ds(0, ff), pl.ds(0, rest)] = wd_raw[layer, pl.ds(0, ff), :]

    def multiply_up(layer, k_range, finish):
        for f in range(strips):
            height = pl.ds(f * MXU, MXU)
            for k in k_range:
                left = x_buf[:, pl.ds(k * MXU, MXU)]
                for i in range(2):
                    _, dst, _, turned = ups[i]
                    if (k + 1) * MXU <= whole:
                        tile = dst[layer, height, pl.ds(k * MXU, MXU)]
                    else:
                        tile = filled(turned[layer, :, height], MXU)
                    register = (f * len(k_range) + k - k_range[0]) % 2
                    pltpu.matmul_push_rhs(tile, staging_register=register, mxu_index=i)
                    pltpu.matmul_acc_lhs(accs[i][f], left, load_staged_rhs=register)
            if finish:
                g = pltpu.matmul_pop(accs[0][f])
                u = pltpu.matmul_pop(accs[1][f])
                value = g * jax.nn.sigmoid(1.702 * g) * (u + 1.0)
                if (f + 1) * MXU > ff:
                    place = lax.broadcasted_iota(jnp.int32, value.shape, 1)
                    value = jnp.where(place < ff - f * MXU, value, 0.0)
                act[:, height] = value.astype(jnp.bfloat16)

    def multiply_down(layer, n):
        acc = accs[n % 2][n // 2 % strips]
        cols = pl.ds(n * MXU, MXU)
        for k in range(strips):
            height = pl.ds(k * MXU, min(MXU, ff - k * MXU))
            tile = wd[layer, height, cols] if (n + 1) * MXU <= whole else wd_rest[layer, height, :]
            pltpu.matmul_push_rhs(filled(tile, MXU), staging_register=k % 2, mxu_index=n % 2)
            pltpu.matmul_acc_lhs(acc, act[:, pl.ds(k * MXU, MXU)], load_staged_rhs=k % 2)
        y = pltpu.matmul_pop(acc)
        width = min(MXU, main + pad - n * MXU)
        lane = n * MXU - main if n * MXU >= main else pad + n * MXU
        y = y.reshape(2, half, MXU)[:, :, :width]
        y_buf[layer, :, :, pl.ds(lane, width)] = y
        y_half[layer, :, :, pl.ds(lane, width)] = y.astype(jnp.bfloat16)

    def number_slots(layer):
        for chip in range(chips):
            count = jnp.int32(0)
            for t in range(rows):
                named = route_nums[layer, t, 0] == chip
                for k in range(1, route_nums.shape[2]):
                    named = named | (route_nums[layer, t, k] == chip)
                slots[layer, chip, t] = jnp.where(named, count, -1)
                count = count + jnp.where(named, 1, 0)

    def pack(layer, chip):
        spots = [slots[layer, chip, t] for t in range(rows)]

        def piece(lane, width, j):
            place = lax.broadcasted_iota(jnp.int32, (rows, width), 0)
            value = jnp.zeros((rows, width), jnp.float32)
            for t in range(rows):
                row = jnp.broadcast_to(norm_buf[t : t + 1, pl.ds(lane, width)], (rows, width))
                value = jnp.where(place == spots[t], row, value)
            if j is not None:
                for t in range(rows):
                    row = jnp.broadcast_to(norm_buf[t : t + 1, pl.ds(main, width)], (rows, width))
                    spot = jnp.where(spots[t] == j, CAP, -1)
                    value = jnp.where(place == spot, row, value)
            return value.astype(jnp.bfloat16)

        pieces = [piece(j * pad, pad, j) for j in range(CAP)]
        if CAP * pad < main:
            pieces.append(piece(CAP * pad, main - CAP * pad, None))
        return jnp.concatenate(pieces, axis=1)

    def unfold(value):
        place = lax.rem(lax.broadcasted_iota(jnp.int32, (8, pad), 0), rows)
        total = jnp.zeros((8, pad), jnp.float32)
        for j in range(CAP):
            moved = pltpu.roll(value[:, j * pad : (j + 1) * pad], 8 + j - CAP, 0)
            total = jnp.where(place == j, moved, total)
        return total

    def fold(part, middle, end):
        c0, cw = parts[part]
        place = lax.rem(lax.broadcasted_iota(jnp.int32, (8, pad), 0), rows)
        pieces = []
        lane = 0
        for j in range(CAP):
            if c0 <= j * pad < c0 + cw:
                moved = pltpu.roll(end, CAP - j, 0)
                pieces.append(jnp.where(place == CAP, moved, middle[:, lane : lane + pad]))
                lane += pad
        if lane < cw:
            pieces.append(middle[:, lane:])
        return jnp.concatenate(pieces, axis=1) if len(pieces) > 1 else pieces[0]

    unrolled = chips <= 16 and chips & (chips - 1) == 0

    def mirror(flip):
        total = 0
        bit = 1
        while bit < chips:
            own = lax.rem(me // bit, 2)
            total = total + bit * (1 - own if flip & bit else own)
            bit *= 2
        return total

    mirrored = [mirror(flip) for flip in range(chips - 1, 0, -1)] if unrolled else []

    def each_peer(body):
        for peer in mirrored:
            body(peer)
        if not unrolled:
            @pl.loop(1, chips)
            def _(d):
                body(lax.rem(me + d, chips))

    def near_peers(body):
        for peer in mirrored[::-1]:
            body(peer)
        if not unrolled:
            each_peer(body)

    def each_group(count, body):
        if fast:
            for q in range(count):
                body(q)
        else:
            pl.loop(0, count)(body)

    def each_chip(body):
        if unrolled:
            for slot in range(chips):
                body(slot)
        else:
            pl.loop(0, chips)(body)

    def gather_copy(layer, cut, half_idx, peer, slot):
        block = gathered.at[layer, half_idx, slot, :, pl.ds(*cuts[cut])]
        return pltpu.make_async_remote_copy(
            src_ref=packed.at[layer, peer] if fast else block,
            dst_ref=block,
            send_sem=ag_send.at[layer, cut, peer],
            recv_sem=ag_recv.at[layer, cut, slot],
            device_id={"expert": peer, "dp": other},
            device_id_type=MESH,
        )

    def forward_copy(layer, cut, half_idx, slot):
        block = gathered.at[layer, half_idx, slot, :, pl.ds(*cuts[cut])]
        return pltpu.make_async_remote_copy(
            src_ref=block,
            dst_ref=block,
            send_sem=fw_send.at[layer, cut, slot],
            recv_sem=fw_recv.at[layer, cut, slot],
            device_id={"dp": other},
            device_id_type=MESH,
        )

    def pair_copy(layer, part):
        c0, cw = pair_lanes[part]
        return pltpu.make_async_remote_copy(
            src_ref=y_half.at[layer, core, :, pl.ds(c0, cw)],
            dst_ref=peer_buf.at[layer, :, pl.ds(c0, cw)],
            send_sem=pr_send.at[layer, part],
            recv_sem=pr_recv.at[layer, part],
            device_id={"dp": other},
            device_id_type=MESH,
        )

    def home_copy(layer, part, peer, slot_src, slot_dst):
        c0, cw = parts[part]
        return pltpu.make_async_remote_copy(
            src_ref=blocks.at[layer, slot_src, :, pl.ds(c0, cw)],
            dst_ref=back.at[layer, slot_dst, :, pl.ds(c0, cw)],
            send_sem=rs_send.at[layer, part, peer],
            recv_sem=rs_recv.at[layer, part, slot_dst],
            device_id={"expert": peer, "dp": other},
            device_id_type=MESH,
        )

    def beside_copy(layer, part):
        c0, cw = parts[part]
        return pltpu.make_async_remote_copy(
            src_ref=blocks.at[layer, me, :, pl.ds(c0, cw)],
            dst_ref=back.at[layer, me, :, pl.ds(c0, cw)],
            send_sem=rs_send.at[layer, part, me],
            recv_sem=rs_recv.at[layer, part, me],
            device_id={"dp": other},
            device_id_type=MESH,
        )

    inputs = [
        pltpu.make_async_copy(src, dst, in_sem.at[i])
        for i, (src, dst) in enumerate(
            ((tok_hbm, tok_ref), (gain_hbm, gain_ref), (routes_hbm, routes_ref), (gates_hbm, gates_ref))
        )
    ]
    if fast:
        inputs.append(pltpu.make_async_copy(routes_hbm, route_nums, in_sem.at[4]))
    for copy in inputs:
        copy.start()
    barrier = pltpu.get_barrier_semaphore()
    each_peer(
        lambda peer: pl.semaphore_signal(
            barrier, inc=1, device_id={"expert": peer, "dp": other}, device_id_type=MESH
        )
    )
    pl.semaphore_signal(barrier, inc=1, device_id={"dp": other}, device_id_type=MESH)
    for copy in inputs:
        copy.wait()
    for copy in weights(0):
        copy.start()

    if fast:
        for layer in range(layers):
            number_slots(layer)
        norm_buf[...] = jnp.zeros_like(norm_buf)
    hidden[...] = tok_ref[...].astype(jnp.float32)
    gains = gain_ref[...].astype(jnp.float32)
    for layer in range(layers):
        x = hidden[...]
        scale_inv = lax.rsqrt(jnp.mean(x * x, axis=-1, keepdims=True) + EPS)
        normed = (x * scale_inv * gains[layer : layer + 1]).astype(jnp.bfloat16)
        if fast:
            norm_buf[:, pl.ds(0, d_model)] = normed.astype(jnp.float32)
        else:
            gathered[layer, core, me] = normed
        if layer == 0:
            if fast:
                for peer in mirrored:
                    packed[layer, peer] = pack(layer, peer)
                gathered[layer, core, me] = pack(layer, me)
            pl.semaphore_wait(barrier, chips)
        for cut in range(len(cuts)):
            def hand_out(peer):
                if fast and layer > 0:
                    packed[layer, peer] = pack(layer, peer)
                gather_copy(layer, cut, core, peer, me).start()

            each_peer(hand_out)
            if fast and layer > 0:
                gathered[layer, core, me] = pack(layer, me)
            forward_copy(layer, cut, core, me).start()
        if layer == 0:
            for later in range(1, layers):
                for copy in weights(later):
                    copy.start()
        if fast:
            turn_all(layer, [(i, f) for f in range(strips) for i in range(2) if layer == 0 or i == 1])
            pad_down(layer)

        for cut in range(len(cuts)):
            def pass_on(peer):
                gather_copy(layer, cut, other, peer, peer).wait_recv()
                forward_copy(layer, cut, other, peer).start()

            near_peers(pass_on)

        per = 8 // rows

        def stack(cut):
            c0, cw = cuts[cut]
            cols = pl.ds(c0, cw)
            def lift(h):
                def one_group(q):
                    value = jnp.concatenate(
                        [
                            gathered[layer, h, q * per + i, :, cols].astype(jnp.float32)
                            for i in range(per)
                        ],
                        axis=0,
                    )
                    stacked[h, q, :, cols] = value
                    if fast:
                        stacked[h, q, :, pl.ds(main, pad)] = unfold(value)

                each_group(chips // per, one_group)
                if fast:
                    height = pl.ds(pl.multiple_of(h * half, half), half)
                    lanes = pl.ds(0, main + pad)
                    x_buf[height, lanes] = (
                        stacked[h].reshape(half, main + pad).astype(jnp.bfloat16)
                    )

            forward_copy(layer, cut, other, me).wait_recv()
            if fast:
                lift(other)
            each_peer(lambda peer: forward_copy(layer, cut, core, peer).wait_recv())
            if fast:
                lift(core)
            else:
                lift(0)
                lift(1)
                x_buf[:, cols] = stacked[:, :, :, cols].reshape(2 * half, cw).astype(jnp.bfloat16)

        if fast:
            short = x_buf.shape[1] - main - pad
            if short and layer == 0:
                x_buf[:, pl.ds(main + pad, short)] = jnp.zeros((2 * half, short), jnp.bfloat16)
        else:
            for cut in range(len(cuts)):
                stack(cut)
            w_gate, w_up, w_down = weights(layer)
            w_gate.wait()
            w_up.wait()

        def up_tile(c0, cw):
            cols = pl.ds(c0, cw)
            g = dot_rows(wg[layer, cols, :], x_buf[...]).T
            u = dot_rows(wu[layer, cols, :], x_buf[...]).T
            act[:, cols] = (g * jax.nn.sigmoid(1.702 * g) * (u + 1.0)).astype(jnp.bfloat16)

        if fast:
            for cut, (c0, cw) in enumerate(cuts):
                stack(cut)
                multiply_up(layer, range(-(-d_model // MXU)), True)
            down_copy(layer).wait()
        else:
            tiled_loop(0, ff, TILE, up_tile)
            w_down.wait()

        def down_tile(c0, cw):
            cols = pl.ds(c0, cw)
            y = jnp.dot(act[...], wd[layer, :, cols], preferred_element_type=jnp.float32)
            y_buf[layer, :, :, cols] = y.reshape(2, half, cw)
            y_half[layer, :, :, cols] = y.reshape(2, half, cw).astype(jnp.bfloat16)

        def send_home(part):
            c0, cw = parts[part]
            cols = pl.ds(c0, cw)
            pair_copy(layer, part).wait_recv()

            def one_group(q):
                group = pl.ds(q * 8 if fast else pl.multiple_of(q * 8, 8), 8)
                def added(lanes):
                    mine, theirs = y_buf[layer, other, group, lanes], peer_buf[layer, group, lanes]
                    return mine + theirs.astype(jnp.float32)

                if fast:
                    total = fold(part, added(pl.ds(pad + c0, cw)), added(pl.ds(0, pad)))
                else:
                    total = added(cols)
                for i in range(per):
                    blocks[layer, q * per + i, :, cols] = total[i * rows : (i + 1) * rows].astype(
                        jnp.bfloat16
                    )

            each_group(chips // per, one_group)
            each_peer(lambda peer: home_copy(layer, part, peer, peer, me).start())
            beside_copy(layer, part).start()

        for part, (c0, cw) in enumerate(parts):
            if fast:
                first = range(main // MXU, -(-d_model // MXU)) if part == 0 else ()
                for n in (*first, *range(c0 // MXU, (c0 + cw) // MXU)):
                    multiply_down(layer, n)
            else:
                tiled_loop(c0, c0 + cw, TILE, down_tile)
            pair_copy(layer, part).start()
            if part > 0 and not fast:
                send_home(part - 1)
        for part in range(len(parts)) if fast else [len(parts) - 1]:
            send_home(part)
        if fast and layer + 1 < layers:
            turn_all(layer + 1, [(0, f) for f in range(strips)])

        routes = routes_ref[layer]
        gates = gates_ref[layer]

        def weight_of(chip):
            expert = chip // chips_per_expert
            return jnp.sum(jnp.where(routes == expert, gates, 0.0), axis=1, keepdims=True)

        def shares_of(chip):
            place = lax.broadcasted_iota(jnp.int32, (rows, 1), 0)
            spot = jnp.full((rows, 1), -1, jnp.int32)
            for t in range(rows):
                spot = jnp.where(place == t, slots[layer, chip, t], spot)
            weight = weight_of(chip)
            return [jnp.where(spot == j, weight, 0.0) for j in range(CAP)]

        def add(chip, shares):
            if not fast:
                hidden[...] += weight_of(chip) * back[layer, chip].astype(jnp.float32)
                return
            block = back[layer, chip].astype(jnp.float32)
            middle = sum(shares[j] * block[j : j + 1] for j in range(CAP))
            end = sum(shares[j] * block[CAP : CAP + 1, j * pad : (j + 1) * pad] for j in range(CAP))
            hidden[:, pl.ds(0, main)] += middle
            hidden[:, pl.ds(main, d_model - main)] += end[:, : d_model - main]

        def take(peer, shares=None):
            for part in range(len(parts)):
                home_copy(layer, part, peer, peer, peer).wait_recv()
            add(peer, shares)

        own = shares_of(me) if fast else None
        known = [shares_of(peer) for peer in mirrored[::-1]] if fast else []
        for part in range(len(parts)):
            beside_copy(layer, part).wait_recv()
        add(me, own)
        if fast:
            for peer, shares in zip(mirrored[::-1], known):
                take(peer, shares)
        else:
            near_peers(take)
        result = hidden[...].astype(jnp.bfloat16)
        if layer + 1 < layers:
            hidden[...] = result.astype(jnp.float32)
        else:
            out_ref[...] = result

    for layer in range(layers):
        for cut in range(len(cuts)):
            each_peer(lambda peer: forward_copy(layer, cut, other, peer).wait_send())
            forward_copy(layer, cut, core, me).wait_send()

        def sent(peer):
            for cut in range(len(cuts)):
                gather_copy(layer, cut, core, peer, me).wait_send()
            for part in range(len(parts)):
                home_copy(layer, part, peer, peer, me).wait_send()

        each_peer(sent)
        for part in range(len(parts)):
            pair_copy(layer, part).wait_send()
            beside_copy(layer, part).wait_send()


def on_device(tokens, norm_gain, w_gate, w_up, w_down, routes, gates, *, expert_total_of):
    chips = lax.axis_size("expert")
    cores = lax.axis_size("dp")
    rows, d_model = tokens.shape
    layers, _, ff = w_gate.shape
    expert_total = expert_total_of(d_model, ff, chips * cores)
    half = chips * rows
    vmem = pl.BlockSpec(memory_space=pltpu.VMEM)
    top = routes.shape[-1]
    hbm = pl.BlockSpec(memory_space=pl.ANY)
    dma = pltpu.SemaphoreType.DMA
    parts = len(col_tiles(0, d_model, -(-d_model // (128 * PARTS)) * 128))
    bf16, f32 = jnp.bfloat16, jnp.float32
    fast = tiled(chips, chips // expert_total, rows, d_model, ff)
    main, pad = folded(d_model) if fast else (d_model, 0)
    lanes = main + pad
    strips = -(-ff // MXU)
    whole, high = d_model // MXU * MXU, strips * MXU
    rest, wide = d_model - whole, -(-d_model // MXU) * MXU
    body = functools.partial(kernel, chips, chips // expert_total)
    if fast:
        ups = [pltpu.VMEM((layers, high, whole), bf16)] * 2 + [pltpu.VMEM((layers, ff, whole), bf16)]
        tails = [pltpu.VMEM((layers, high, rest), bf16)] * 3
        tails += [pltpu.VMEM((layers, rest, high), bf16)] * 2 + [pltpu.VMEM((layers, high, MXU), bf16)]
        tails += [
            pltpu.VMEM((layers, chips, rows, main), bf16),
            pltpu.VMEM((rows, lanes), f32),
            pltpu.SMEM((layers, rows, top), jnp.int32),
            pltpu.SMEM((layers, chips, rows), jnp.int32),
        ]
        x_shape, act_shape, w_sems = (2 * half, wide), (2 * half, high), (layers, 3, strips + 1)

        def body(*refs):
            each = [pltpu.ACC(i)((2 * half, MXU), f32) for i in range(2) for _ in range(strips)]
            pl.run_scoped(
                lambda *accs: kernel(
                    chips, chips // expert_total, *refs, accs=(accs[:strips], accs[strips:])
                ),
                *each,
            )
    else:
        ups, tails = [pltpu.VMEM((layers, ff, d_model), bf16)] * 3, []
        x_shape, act_shape, w_sems = (2 * half, d_model), (2 * half, ff), (layers, 3)
    return pl.pallas_call(
        body,
        out_shape=jax.ShapeDtypeStruct(tokens.shape, tokens.dtype),
        in_specs=[hbm] * 7,
        out_specs=vmem,
        scratch_shapes=[
            *ups,
            pltpu.VMEM((layers, 2, chips, rows, main), bf16),
            pltpu.VMEM((2, half // 8, 8, lanes), f32),
            pltpu.VMEM(x_shape, bf16),
            pltpu.VMEM(act_shape, bf16),
            pltpu.VMEM((layers, 2, half, lanes), f32),
            pltpu.VMEM((layers, 2, half, lanes), bf16),
            pltpu.VMEM((layers, half, lanes), bf16),
            pltpu.VMEM((layers, chips, rows, main), bf16),
            pltpu.VMEM((layers, chips, rows, main), bf16),
            pltpu.VMEM((rows, d_model), f32),
            dma(w_sems),
            dma((layers, CUTS, chips)),
            dma((layers, CUTS, chips)),
            dma((layers, CUTS, chips)),
            dma((layers, CUTS, chips)),
            dma((layers, parts)),
            dma((layers, parts)),
            dma((layers, parts, chips)),
            dma((layers, parts, chips)),
            pltpu.VMEM((rows, d_model), bf16),
            pltpu.VMEM((layers, d_model), bf16),
            pltpu.VMEM((layers, rows, top), jnp.int32),
            pltpu.VMEM((layers, rows, top), f32),
            dma((5,)),
            *tails,
        ],
        compiler_params=pltpu.CompilerParams(
            collective_id=0, has_side_effects=True, vmem_limit_bytes=67043328
        ),
    )(
        tokens,
        norm_gain,
        jnp.swapaxes(w_gate, 1, 2),
        jnp.swapaxes(w_up, 1, 2),
        w_down,
        routes,
        gates,
    )


def solution(mesh):
    def expert_total_of(d_model, ff, devices):
        return devices * ff // d_model

    return jax.shard_map(
        functools.partial(on_device, expert_total_of=expert_total_of),
        mesh=mesh,
        in_specs=(
            P(("groups", "expert", "dp"), None),
            P(),
            P(None, None, ("expert", "dp")),
            P(None, None, ("expert", "dp")),
            P(None, ("expert", "dp"), None),
            P(None, ("groups", "expert", "dp"), None),
            P(None, ("groups", "expert", "dp"), None),
        ),
        out_specs=P(("groups", "expert", "dp"), None),
        check_vma=False,
    )
```

profile of v0, /device:TPU:0, one launch (start us, length us, event | category | flops | bytes accessed | tf_op | source)
XLA Modules:
  0.0 43.9 jit_solution(11959283907558427896)
XLA Ops:
  0.0 42.5 %shard_map.73 = bf16[4,2880]{1,0:T(4,128)(2,1)} custom-call(bf16[4,2880]{1,0:T(4,128)(2,1)} %refs_0_.1, bf16[2,2880]{1,0:T(2,128)(2,1)} %refs_1_.1, bf16[2,1440,2880]{2,1,0:T(8,128)(2,1)} %bitcast.2, bf16[2,1440,2880]{2,1,0:T(8,128)(2,1)} %bitcast.3, bf16[2,1440,2880]{2,1,0:T(8,128)(2,1)} %refs_4_.1, s32[2,4,4]{2,1,0:T(4,128)} %refs_5_.1, f32[2,4,4]{2,1,0:T(4,128)} %refs_6_.1), custom_call_target="tpu_custom_call" | custom-call | tf_op jit(solution)/shard_map/pallas_call | solution.py:630
  42.5 1.4 %copy.9 = bf16[4,2880]{1,0:T(4,128)(2,1)} copy(bf16[4,2880]{1,0:T(4,128)(2,1)} %shard_map.73) | data formatting | bytes 46080
where the time goes:
time: 44.1 us; the launch traced here: 43.9 us
  Pallas kernels  42.5 us (96%)
  local copies, waits for them, and re-layouts  1.35 us (3%)
    pallas_call x1, Pallas kernels, on_device(): pl.pallas_call(body, out_shape=jax.ShapeDtypeStruct(tokens.shape, tokens....  42.5 us
    unnamed x1, local copies, waits for them, and re-layouts  1.35 us

commit v1 on v0

--- a/solution.py
+++ b/solution.py
@@ -369,8 +369,7 @@
         copy.start()
 
     if fast:
-        for layer in range(layers):
-            number_slots(layer)
+        number_slots(0)
         norm_buf[...] = jnp.zeros_like(norm_buf)
     hidden[...] = tok_ref[...].astype(jnp.float32)
     gains = gain_ref[...].astype(jnp.float32)
@@ -398,6 +397,8 @@
             if fast and layer > 0:
                 gathered[layer, core, me] = pack(layer, me)
             forward_copy(layer, cut, core, me).start()
+        if fast and layer + 1 < layers:
+            number_slots(layer + 1)
         if layer == 0:
             for later in range(1, layers):
                 for copy in weights(later):
@@ -419,6 +420,8 @@
             c0, cw = cuts[cut]
             cols = pl.ds(c0, cw)
             def lift(h):
+                whole_rows, end_rows = [], []
+
                 def one_group(q):
                     value = jnp.concatenate(
                         [
@@ -427,17 +430,17 @@
                         ],
                         axis=0,
                     )
-                    stacked[h, q, :, cols] = value
                     if fast:
-                        stacked[h, q, :, pl.ds(main, pad)] = unfold(value)
+                        whole_rows.append(value)
+                        end_rows.append(unfold(value))
+                    else:
+                        stacked[h, q, :, cols] = value
 
                 each_group(chips // per, one_group)
                 if fast:
                     height = pl.ds(pl.multiple_of(h * half, half), half)
-                    lanes = pl.ds(0, main + pad)
-                    x_buf[height, lanes] = (
-                        stacked[h].reshape(half, main + pad).astype(jnp.bfloat16)
-                    )
+                    for lanes, found in ((cols, whole_rows), (pl.ds(main, pad), end_rows)):
+                        x_buf[height, lanes] = jnp.concatenate(found, axis=0).astype(jnp.bfloat16)
 
             forward_copy(layer, cut, other, me).wait_recv()
             if fast:

time: 44.1 us -> 44.2 us (level)
  no operation moved by 1% of the time
where the time goes in v1:
time: 44.2 us; the launch traced here: 44 us
  Pallas kernels  42.6 us (96%)
  local copies, waits for them, and re-layouts  1.35 us (3%)
    pallas_call x1, Pallas kernels, on_device(): pl.pallas_call(body, out_shape=jax.ShapeDtypeStruct(tokens.shape, tokens....  42.6 us
    unnamed x1, local copies, waits for them, and re-layouts  1.35 us

profile of v1, /device:TPU:0, one launch (start us, length us, event | category | flops | bytes accessed | tf_op | source)
XLA Modules:
  0.0 44.0 jit_solution(9108047202304888810)
XLA Ops:
  0.0 42.6 %shard_map.73 = bf16[4,2880]{1,0:T(4,128)(2,1)} custom-call(bf16[4,2880]{1,0:T(4,128)(2,1)} %refs_0_.1, bf16[2,2880]{1,0:T(2,128)(2,1)} %refs_1_.1, bf16[2,1440,2880]{2,1,0:T(8,128)(2,1)} %bitcast.2, bf16[2,1440,2880]{2,1,0:T(8,128)(2,1)} %bitcast.3, bf16[2,1440,2880]{2,1,0:T(8,128)(2,1)} %refs_4_.1, s32[2,4,4]{2,1,0:T(4,128)} %refs_5_.1, f32[2,4,4]{2,1,0:T(4,128)} %refs_6_.1), custom_call_target="tpu_custom_call" | custom-call | tf_op jit(solution)/shard_map/pallas_call | solution.py:633
  42.6 1.4 %copy.9 = bf16[4,2880]{1,0:T(4,128)(2,1)} copy(bf16[4,2880]{1,0:T(4,128)(2,1)} %shard_map.73) | data formatting | bytes 46080
